TPU v7x, 512 devices: a 8x2x16 block of a 8x16x16 slice. The times are simulated.
512 devices in a mesh: ckpt: 2 (over y), row: 32 (over z, core), col: 8 (over x).
Axes of the slice: x: 8, y: 2, z: 16, core: 2. Of those that a mesh axis runs over, the one named last changes fastest.
The devices are a block of a 8x16x16 slice.
Arguments:
- grad_slab: bfloat16 [768, 27648], P(('ckpt', 'col'), 'row'), parts along dimension 0, may hold values from -6 to 6
- eigenbasis: bfloat16 [55296, 14336], P(('ckpt', 'row'), 'col'), parts along dimension 0, may hold values from -0.0625 to 0.0625
- eigenvalues: bfloat16 [768, 14336], P('ckpt', 'col'), parts along dimension 0, may hold values from 0.049804688 to 5
Outputs:
- preconditioned: bfloat16 [768, 27648], P(('ckpt', 'col'), 'row'), parts along dimension 0
There are 2 independent parts, one for each index of `ckpt`. A program takes and returns all parts, laid end to end along the dimension named above; each array names one. Nothing has to cross between parts.
All inputs are finite; a program needn't handle non-finite values.
Results may differ from a plain program's by a relative error of at most 0.0046.
Values may be sent and summed in bfloat16 or wider, within the bound.
A program may use at most 64 MiB of HBM per device.

v0:
```python
import jax
import jax.numpy as jnp
from jax import lax
from jax.sharding import Mesh
from jax.sharding import PartitionSpec as P

ROW = ("row_0", "row_1")
CKPT_ROW = ("ckpt", "row_0", "row_1")
DAMPING = 0.1


def laid_out(blocks, dim):
    blocks = jnp.moveaxis(blocks, 0, dim)
    lengths = blocks.shape
    return blocks.reshape(*lengths[:dim], lengths[dim] * lengths[dim + 1], *lengths[dim + 2 :])


def copy_for_each(value, axis):
    copies = jnp.broadcast_to(value, (lax.axis_size(axis), *value.shape))
    return lax.all_to_all(copies, axis, split_axis=0, concat_axis=0, tiled=True)


def gather_directly(value, axis, dim):
    return laid_out(copy_for_each(value, axis), dim)


def reduced_to_own(blocks, axes, order):
    inside = blocks.shape[1:]
    blocks = blocks.reshape(*(lax.axis_size(a) for a in axes), *inside)
    blocks = jnp.moveaxis(blocks, order, range(len(axes))).reshape(-1, *inside)
    for k in order:
        blocks = lax.psum_scatter(blocks, axes[k], scatter_dimension=0, tiled=True)
    return blocks[0]


def split_up(value, dim, count):
    before, after = (value.shape[:dim], value.shape[dim + 1 :])
    return jnp.moveaxis(value.reshape(*before, count, -1, *after), dim, 0)


def scatter_axes(value, axes, order, dim):
    count = lax.axis_size(axes)
    return reduced_to_own(split_up(value, dim, count), axes, order)


def all_blocks(value, axes, order):
    blocks = value[None]
    for k in order:
        blocks = lax.all_gather(blocks, axes[k], axis=0, tiled=True)
    carried = [lax.axis_size(axes[k]) for k in reversed(order)]
    blocks = blocks.reshape(*carried, *value.shape)
    turned = sorted(range(len(order)), key=lambda place: order[len(order) - 1 - place])
    return blocks.transpose(*turned, *range(len(order), blocks.ndim)).reshape(-1, *value.shape)


def whole_of(value, axes, order, dim):
    return laid_out(all_blocks(value, axes, order), dim)


def summed_on_arrival(value, axis, dim):
    count = lax.axis_size(axis)
    blocks = lax.all_to_all(split_up(value, dim, count), axis, 0, 0, tiled=True)
    return jnp.sum(blocks, axis=0)


def on_device(grad_slab, eigenbasis, eigenvalues):
    rotated_part = jnp.dot(
        gather_directly(grad_slab, "col", 0), eigenbasis, preferred_element_type=jnp.float32
    )
    own_share = scatter_axes(rotated_part, ROW, (1, 0), 1)
    share_width = own_share.shape[1]
    offset = lax.axis_index(ROW) * share_width
    own_values = lax.dynamic_slice_in_dim(eigenvalues, offset, share_width, 1)
    scaled_share = (own_share / (own_values.astype(jnp.float32) + DAMPING)).astype(jnp.bfloat16)
    scaled = whole_of(scaled_share, ROW, (0, 1), 1)
    result = summed_on_arrival(
        lax.dot_general(
            scaled, eigenbasis, (((1,), (1,)), ((), ())), preferred_element_type=jnp.float32
        ),
        "col",
        0,
    )
    return result.astype(jnp.bfloat16)


def solution(mesh):
    torus = Mesh(
        mesh.devices.reshape(mesh.shape["ckpt"], 16, 2, mesh.shape["col"]),
        ("ckpt", "row_0", "row_1", "col"),
    )
    return jax.shard_map(
        on_device,
        mesh=torus,
        in_specs=(P(("ckpt", "col"), ROW), P(CKPT_ROW, "col"), P("ckpt", "col")),
        out_specs=P(("ckpt", "col"), ROW),
        check_vma=False,
    )
```

profile of v0, /device:TPU:65, one launch (start us, length us, event | category | flops | bytes accessed | tf_op | source)
XLA Modules:
  0.0 314.1 jit_solution(3465347139622952609)
XLA Ops:
  6.5 1.8 broadcast_in_dim.6
  8.3 7.9 %all-to-all-start = ((bf16[8,48,864]{2,1,0:T(8,128)(2,1)}), bf16[8,48,864]{2,1,0:T(8,128)(2,1)}, u32[]{:S(2)}, u32[]{:S(2)}) async-start(bf16[8,48,864]{2,1,0:T(8,128)(2,1)} %broadcast_in_dim.6), calls=%async_computation | async-start | bytes 1376256 | tf_op jit(solution)/shard_map/all_to_all | solution.py:20
  16.2 0.1 reduce-scatter.3.cloned.1.call-start
  16.3 4.5 %copy.16 = bf16[864,1792]{0,1:T(8,128)(2,1)S(1)} copy(bf16[864,1792]{1,0:T(8,128)(2,1)} %param.4) | data formatting | bytes 6193152 | tf_op args[1]
  20.8 9.4 %all-to-all-done = bf16[8,48,864]{2,1,0:T(8,128)(2,1)} async-done(((bf16[8,48,864]{2,1,0:T(8,128)(2,1)}), bf16[8,48,864]{2,1,0:T(8,128)(2,1)}, u32[]{:S(2)}, u32[]{:S(2)}) %all-to-all-start) | async-done | bytes 663584 | tf_op jit(solution)/shard_map/all_to_all | solution.py:20
  30.2 4.8 %fusion.3 = f32[384,32,56]{0,2,1:T(8,128)} fusion(bf16[384,864,1]{1,0,2:T(8,128)(2,1)} %bitcast.1, bf16[32,56,864]{2,1,0:T(8,128)(2,1)S(1)} %bitcast.32), kind=kOutput, calls=%fused_computation.4 | convolution fusion | flops 1189085184 | bytes 6512640 | tf_op jit(solution)/shard_map/dot_general | solution.py:67
  35.1 5.6 %copy.18 = f32[2,16,384,56]{3,2,1,0:T(8,128)} copy(f32[2,16,384,56]{2,3,0,1:T(8,128)} %bitcast.33) | data formatting | bytes 5505024 | tf_op jit(solution)/shard_map/transpose | solution.py:30
  40.7 0.1 reduce-scatter.3.cloned.1.call-update
  40.7 0.1 reduce-scatter.5.cloned.1.call-start
  40.8 64.1 %reduce-scatter.3.cloned.1.call-done = f32[16,384,56]{2,1,0:T(8,128)} async-done(((f32[32,384,56]{2,1,0:T(8,128)}), f32[16,384,56]{2,1,0:T(8,128)}) %reduce-scatter.3.cloned.1.call-update) | async-done | bytes 1376272 | tf_op jit(solution)/shard_map/reduce_scatter | solution.py:32
  104.9 0.1 reduce-scatter.5.cloned.1.call-update
  104.9 0.1 all-gather.3.cloned.1.call-start
  105.0 73.0 %reduce-scatter.5.cloned.1.call-done = f32[1,384,56]{2,1,0:T(8,128)} async-done(((f32[16,384,56]{2,1,0:T(8,128)}), f32[1,384,56]{2,1,0:T(8,128)}) %reduce-scatter.5.cloned.1.call-update) | async-done | bytes 86032 | tf_op jit(solution)/shard_map/reduce_scatter | solution.py:32
  178.0 1.1 fusion.2
  179.1 30.7 %all-gather = bf16[6144,56]{1,0:T(8,128)(2,1)S(1)} all-gather(bf16[384,56]{1,0:T(8,128)(2,1)S(1)} %fusion.2), channel_id=2, replica_groups=mesh['ckpt'=2,'row_0'=16,'row_1'=2,'col'=8] {'row_0'}, dimensions={0}, use_global_device_ids=true | all-gather | bytes 731136 | tf_op jit(solution)/shard_map/all_gather | solution.py:49
  209.8 1.4 copy.20
  211.2 0.1 all-gather.3.cloned.1.call-update
  211.3 38.6 %all-gather.3.cloned.1.call-done = bf16[32,384,56]{1,2,0:T(8,128)(2,1)} async-done(((bf16[16,384,56]{1,2,0:T(8,128)(2,1)}), bf16[32,384,56]{1,2,0:T(8,128)(2,1)}) %all-gather.3.cloned.1.call-update) | async-done | bytes 1376272 | tf_op jit(solution)/shard_map/all_gather | solution.py:49
  249.9 7.0 %copy.21 = bf16[16,2,384,56]{3,1,0,2:T(2,128)(2,1)S(1)} copy(bf16[16,2,384,56]{2,3,0,1:T(8,128)(2,1)} %bitcast.34) | data formatting | bytes 2752512 | tf_op jit(solution)/shard_map/transpose | solution.py:53
  256.9 6.5 %dot_general.15 = bf16[8,48,1792]{2,1,0:T(8,128)(2,1)} reshape(bf16[384,32,56]{2,1,0:T(8,128)(2,1)S(1)} %bitcast.30) | data formatting | bytes 2752512 | tf_op jit(solution)/shard_map/dot_general | solution.py:77
  263.4 3.9 %fusion = f32[8,48,864]{2,1,0:T(8,128)S(1)} fusion(bf16[8,48,1792]{2,1,0:T(8,128)(2,1)} %dot_general.15, bf16[864,1792]{1,0:T(8,128)(2,1)} %param.4), kind=kOutput, calls=%fused_computation | convolution fusion | flops 1189085184 | bytes 5799936 | tf_op jit(solution)/shard_map/dot_general | solution.py:77
  267.3 39.6 %all_to_all.10 = f32[8,48,864]{2,1,0:T(8,128)S(1)} all-to-all(f32[8,48,864]{2,1,0:T(8,128)S(1)} %fusion), channel_id=1, replica_groups=mesh['ckpt'=2,'row_0'=16,'row_1'=2,'col'=8] {'col'}, dimensions={0} | all-to-all | bytes 2654208 | tf_op jit(solution)/shard_map/all_to_all | solution.py:62
  306.9 0.7 reduce_sum.9
Async XLA Ops:
  8.3 21.9 %all-to-all-start = ((bf16[8,48,864]{2,1,0:T(8,128)(2,1)}), bf16[8,48,864]{2,1,0:T(8,128)(2,1)}, u32[]{:S(2)}, u32[]{:S(2)}) async-start(bf16[8,48,864]{2,1,0:T(8,128)(2,1)} %broadcast_in_dim.6), calls=%async_computation | async-start | bytes 1376256 | tf_op jit(solution)/shard_map/all_to_all | solution.py:20
  16.2 88.7 %reduce-scatter.3.cloned.1.call-start = ((), (), s32[]{:S(2)}) async-start(), calls=%async_computation.4 | async-start | bytes 9437184 | tf_op jit(solution)/shard_map/reduce_scatter | solution.py:32
  40.7 137.3 %reduce-scatter.5.cloned.1.call-start = ((), (), s32[]{:S(2)}) async-start(), calls=%async_computation.5 | async-start | bytes 3342336 | tf_op jit(solution)/shard_map/reduce_scatter | solution.py:32
  104.9 144.9 %all-gather.3.cloned.1.call-start = ((), (), s32[]{:S(2)}) async-start(), calls=%async_computation.6 | async-start | bytes 2064384 | tf_op jit(solution)/shard_map/all_gather | solution.py:49
Sparse Core Ops, SparseCore 0:
  40.9 63.9 reduce-scatter.2
  107.7 70.2 reduce-scatter.4
  211.4 38.4 all-gather.2
where the time goes:
time: 315 us; the launch traced here: 314 us
  waiting for transfers between devices  185 us (59%)
  blocking collectives  70.3 us (22%)
  local copies, waits for them, and re-layouts  26.9 us (9%)
  between operations  13.2 us (4%)
  matrix products  8.71 us (3%)
  starting transfers between devices  8.04 us (3%)
    reduce_scatter x2, waiting for transfers between devices, reduced_to_own(): blocks = lax.psum_scatter(blocks, axes[k], scatter_dimension=0, tiled=True)  137 us
    all_to_all x1, blocking collectives, summed_on_arrival(): blocks = lax.all_to_all(split_up(value, dim, count), axis, 0, 0, tiled=True)  39.6 us
    all_gather x1, waiting for transfers between devices, all_blocks(): blocks = lax.all_gather(blocks, axes[k], axis=0, tiled=True)  38.6 us
    all_gather x1, blocking collectives, all_blocks(): blocks = lax.all_gather(blocks, axes[k], axis=0, tiled=True)  30.7 us
    all_to_all x1, waiting for transfers between devices, copy_for_each(): return lax.all_to_all(copies, axis, split_axis=0, concat_axis=0, tiled=True)  9.44 us
    all_to_all x1, starting transfers between devices, copy_for_each(): return lax.all_to_all(copies, axis, split_axis=0, concat_axis=0, tiled=True)  7.86 us
    transpose x1, local copies, waits for them, and re-layouts, all_blocks(): blocks.transpose(*turned, *range(len(order), blocks.ndim))  7 us
    dot_general x1, local copies, waits for them, and re-layouts, on_device(): lax.dot_general(scaled, eigenbasis, (((1,), (1,)), ((), ())), preferred_e...  6.53 us
  transfers between devices with their start and end apart: 4, of which 4 were waited for; matrix products, arithmetic and copies ran while one was open for 1% of the time, Pallas kernels for 0%

commit v1 on v0

--- a/solution.py
+++ b/solution.py
@@ -46,7 +46,9 @@
 def all_blocks(value, axes, order):
     blocks = value[None]
     for k in order:
-        blocks = lax.all_gather(blocks, axes[k], axis=0, tiled=True)
+        blocks = jnp.concatenate(
+            lax.all_to_all(jnp.stack([blocks] * lax.axis_size(axes[k])), axes[k], 0, 0), axis=0
+        )
     carried = [lax.axis_size(axes[k]) for k in reversed(order)]
     blocks = blocks.reshape(*carried, *value.shape)
     turned = sorted(range(len(order)), key=lambda place: order[len(order) - 1 - place])

time: 315 us -> 298 us (0.946)
  waiting for transfers between devices: 185 us -> 147 us
  blocking collectives: 70.3 us -> 93.6 us
    all_to_all x0 -> x2, blocking collectives: none -> 51.3 us  [all_blocks(): lax.all_to_all(jnp.stack([blocks] * lax.axis_size(axes[k])), axes[k], 0, 0)]
    all_gather x1 -> x0, waiting for transfers between devices: 38.6 us -> none  [all_blocks(): blocks = lax.all_gather(blocks, axes[k], axis=0, tiled=True)]
    all_gather x1 -> x0, blocking collectives: 30.7 us -> none  [all_blocks(): blocks = lax.all_gather(blocks, axes[k], axis=0, tiled=True)]
    transpose x1, local copies, waits for them, and re-layouts: 7 us -> 1.22 us  [all_blocks(): blocks.transpose(*turned, *range(len(order), blocks.ndim))]
    transpose x0 -> x1, local copies, waits for them, and re-layouts: none -> 5.34 us  [laid_out(): blocks = jnp.moveaxis(blocks, 0, dim)]
  transfers between devices with their start and end apart: 4 -> 3, of which waited for: 4 -> 3; matrix products, arithmetic and copies ran while one was open for 1% -> 2% of each run, Pallas kernels for 0% -> 0%
where the time goes in v1:
time: 298 us
  waiting for transfers between devices  147 us (49%)
  blocking collectives  93.6 us (31%)
  local copies, waits for them, and re-layouts  25.2 us (8%)
  between operations  13.5 us (5%)
  matrix products  8.7 us (3%)
  starting transfers between devices  7.98 us (3%)
    reduce_scatter x2, waiting for transfers between devices, reduced_to_own(): blocks = lax.psum_scatter(blocks, axes[k], scatter_dimension=0, tiled=True)  137 us
    all_to_all x2, blocking collectives, all_blocks(): lax.all_to_all(jnp.stack([blocks] * lax.axis_size(axes[k])), axes[k], 0, 0)  51.3 us
    all_to_all x1, blocking collectives, summed_on_arrival(): blocks = lax.all_to_all(split_up(value, dim, count), axis, 0, 0, tiled=True)  42.3 us
    all_to_all x1, waiting for transfers between devices, copy_for_each(): return lax.all_to_all(copies, axis, split_axis=0, concat_axis=0, tiled=True)  9.44 us
    all_to_all x1, starting transfers between devices, copy_for_each(): return lax.all_to_all(copies, axis, split_axis=0, concat_axis=0, tiled=True)  7.86 us
    dot_general x1, local copies, waits for them, and re-layouts, on_device(): lax.dot_general(scaled, eigenbasis, (((1,), (1,)), ((), ())), preferred_e...  6.53 us
  transfers between devices with their start and end apart: 3, of which 3 were waited for; matrix products, arithmetic and copies ran while one was open for 2% of the time, Pallas kernels for 0%

profile of v1, /device:TPU:65, one launch (start us, length us, event | category | flops | bytes accessed | tf_op | source)
XLA Modules:
  0.0 297.7 jit_solution(16998039325422317722)
XLA Ops:
  6.5 1.8 broadcast_in_dim.3
  8.3 7.9 %all-to-all-start = ((bf16[8,48,864]{2,1,0:T(8,128)(2,1)}), bf16[8,48,864]{2,1,0:T(8,128)(2,1)}, u32[]{:S(2)}, u32[]{:S(2)}) async-start(bf16[8,48,864]{2,1,0:T(8,128)(2,1)} %broadcast_in_dim.3), calls=%async_computation | async-start | bytes 1376256 | tf_op jit(solution)/shard_map/all_to_all | solution.py:20
  16.2 0.1 reduce-scatter.3.cloned.1.call-start
  16.3 4.5 %copy.11 = bf16[864,1792]{0,1:T(8,128)(2,1)S(1)} copy(bf16[864,1792]{1,0:T(8,128)(2,1)} %param.4) | data formatting | bytes 6193152 | tf_op args[1]
  20.8 9.4 %all-to-all-done = bf16[8,48,864]{2,1,0:T(8,128)(2,1)} async-done(((bf16[8,48,864]{2,1,0:T(8,128)(2,1)}), bf16[8,48,864]{2,1,0:T(8,128)(2,1)}, u32[]{:S(2)}, u32[]{:S(2)}) %all-to-all-start) | async-done | bytes 663584 | tf_op jit(solution)/shard_map/all_to_all | solution.py:20
  30.2 4.8 %fusion.3 = f32[384,32,56]{0,2,1:T(8,128)} fusion(bf16[384,864,1]{1,0,2:T(8,128)(2,1)} %bitcast.1, bf16[32,56,864]{2,1,0:T(8,128)(2,1)S(1)} %bitcast.30), kind=kOutput, calls=%fused_computation.5 | convolution fusion | flops 1189085184 | bytes 6512640 | tf_op jit(solution)/shard_map/dot_general | solution.py:69
  35.0 5.6 %copy.13 = f32[2,16,384,56]{3,2,1,0:T(8,128)} copy(f32[2,16,384,56]{2,3,0,1:T(8,128)} %bitcast.31) | data formatting | bytes 5505024 | tf_op jit(solution)/shard_map/transpose | solution.py:30
  40.7 0.1 reduce-scatter.3.cloned.1.call-update
  40.7 0.1 reduce-scatter.5.cloned.1.call-start
  40.8 64.1 %reduce-scatter.3.cloned.1.call-done = f32[16,384,56]{2,1,0:T(8,128)} async-done(((f32[32,384,56]{2,1,0:T(8,128)}), f32[16,384,56]{2,1,0:T(8,128)}) %reduce-scatter.3.cloned.1.call-update) | async-done | bytes 1376272 | tf_op jit(solution)/shard_map/reduce_scatter | solution.py:32
  104.9 0.1 reduce-scatter.5.cloned.1.call-update
  104.9 73.1 %reduce-scatter.5.cloned.1.call-done = f32[1,384,56]{2,1,0:T(8,128)} async-done(((f32[16,384,56]{2,1,0:T(8,128)}), f32[1,384,56]{2,1,0:T(8,128)}) %reduce-scatter.5.cloned.1.call-update) | async-done | bytes 86032 | tf_op jit(solution)/shard_map/reduce_scatter | solution.py:32
  178.0 1.1 fusion.2
  179.1 0.1 copy.14
  179.2 0.1 stack.6
  179.3 32.5 %all_to_all.20 = bf16[16,1,384,56]{2,3,1,0:T(8,128)(2,1)S(1)} all-to-all(bf16[16,1,384,56]{2,3,1,0:T(8,128)(2,1)S(1)} %stack.6), channel_id=1, replica_groups=mesh['ckpt'=2,'row_0'=16,'row_1'=2,'col'=8] {'row_0'}, dimensions={0} | all-to-all | bytes 1376256 | tf_op jit(solution)/shard_map/all_to_all | solution.py:50
  211.8 0.2 pad_maximum_fusion
  212.0 18.8 %all_to_all.21 = bf16[2,16,384,56]{2,3,1,0:T(8,128)(2,1)S(1)} all-to-all(bf16[2,16,384,56]{2,3,1,0:T(8,128)(2,1)S(1)} %pad_maximum_fusion), channel_id=1, replica_groups=mesh['ckpt'=2,'row_0'=16,'row_1'=2,'col'=8] {'row_1'}, dimensions={0} | all-to-all | bytes 2752512 | tf_op jit(solution)/shard_map/all_to_all | solution.py:50
  230.8 1.2 copy.15
  232.0 5.3 %copy.16 = bf16[384,32,56]{2,1,0:T(8,128)(2,1)S(1)} copy(bf16[384,32,56]{0,2,1:T(8,128)(2,1)} %bitcast.29) | data formatting | bytes 2752512 | tf_op jit(solution)/shard_map/transpose | solution.py:13
  237.4 6.5 %dot_general.15 = bf16[8,48,1792]{2,1,0:T(8,128)(2,1)} reshape(bf16[384,32,56]{2,1,0:T(8,128)(2,1)S(1)} %copy.16) | data formatting | bytes 2752512 | tf_op jit(solution)/shard_map/dot_general | solution.py:79
  243.9 3.9 %fusion = f32[8,48,864]{2,1,0:T(8,128)S(1)} fusion(bf16[8,48,1792]{2,1,0:T(8,128)(2,1)} %dot_general.15, bf16[864,1792]{1,0:T(8,128)(2,1)} %param.4), kind=kOutput, calls=%fused_computation | convolution fusion | flops 1189085184 | bytes 5799936 | tf_op jit(solution)/shard_map/dot_general | solution.py:79
  247.8 42.3 %all_to_all.22 = f32[8,48,864]{2,1,0:T(8,128)S(1)} all-to-all(f32[8,48,864]{2,1,0:T(8,128)S(1)} %fusion), channel_id=1, replica_groups=mesh['ckpt'=2,'row_0'=16,'row_1'=2,'col'=8] {'col'}, dimensions={0} | all-to-all | bytes 2654208 | tf_op jit(solution)/shard_map/all_to_all | solution.py:64
  290.1 0.7 reduce_sum.9
Async XLA Ops:
  8.3 21.9 %all-to-all-start = ((bf16[8,48,864]{2,1,0:T(8,128)(2,1)}), bf16[8,48,864]{2,1,0:T(8,128)(2,1)}, u32[]{:S(2)}, u32[]{:S(2)}) async-start(bf16[8,48,864]{2,1,0:T(8,128)(2,1)} %broadcast_in_dim.3), calls=%async_computation | async-start | bytes 1376256 | tf_op jit(solution)/shard_map/all_to_all | solution.py:20
  16.2 88.7 %reduce-scatter.3.cloned.1.call-start = ((), (), s32[]{:S(2)}) async-start(), calls=%async_computation.6 | async-start | bytes 9437184 | tf_op jit(solution)/shard_map/reduce_scatter | solution.py:32
  40.7 137.3 %reduce-scatter.5.cloned.1.call-start = ((), (), s32[]{:S(2)}) async-start(), calls=%async_computation.7 | async-start | bytes 3342336 | tf_op jit(solution)/shard_map/reduce_scatter | solution.py:32
Sparse Core Ops, SparseCore 0:
  40.8 63.9 reduce-scatter.2
  107.7 70.2 reduce-scatter.4
